TPU v7x, 32 devices: a whole 2x2x4 slice. The times are simulated.
32 devices in a mesh: dp: 2 (over x), tp: 4 (over z), kvp: 4 (over y, core).
Axes of the slice: x: 2, y: 2, z: 4, core: 2. Of those that a mesh axis runs over, the one named last changes fastest.
Arguments:
- x_in: bfloat16 [64, 5120], P('dp'), parts along dimension 0
- ctx_len: int32 [64], P('dp'), parts along dimension 0
- g_attn: bfloat16 [5120], replicated
- g_mlp: bfloat16 [5120], replicated
- w_qkv: bfloat16 [5120, 7168], P(None, 'tp')
- w_o: bfloat16 [5120, 5120], P(('tp', 'kvp'))
- w_gate: bfloat16 [5120, 27648], P(None, ('tp', 'kvp'))
- w_up: bfloat16 [5120, 27648], P(None, ('tp', 'kvp'))
- w_down: bfloat16 [27648, 5120], P(('tp', 'kvp'))
- k_cache: bfloat16 [64, 1024, 8, 128], P('dp', 'kvp', 'tp'), parts along dimension 0
- v_cache: bfloat16 [64, 1024, 8, 128], P('dp', 'kvp', 'tp'), parts along dimension 0
Outputs:
- output 1: bfloat16 [64, 5120], P('dp'), parts along dimension 0
- output 2: bfloat16 [64, 1024, 8, 128], P('dp', 'kvp', 'tp'), parts along dimension 0
- output 3: bfloat16 [64, 1024, 8, 128], P('dp', 'kvp', 'tp'), parts along dimension 0
There are 2 independent parts. A program takes and returns all parts, laid end to end along the dimension named above; an argument that names none is the same for every part.
All inputs are finite; a program needn't handle non-finite values.
Results may differ from a plain program's by a relative error of at most 0.00833289.
Values sent between devices are 32-bit elements.
A program may use at most 1 GiB of HBM per device.

v0:
```python
import jax
import jax.numpy as jnp
from jax import lax
from jax.sharding import PartitionSpec as P

ROPE_THETA = 500000.0
EPS = 1e-5
NEG_FILL = -1e30


def rms_norm(values, gain_vec):
    x_f32 = values.astype(jnp.float32)
    inv_rms = lax.rsqrt(jnp.mean(x_f32 * x_f32, axis=-1, keepdims=True) + EPS)
    return (x_f32 * inv_rms * gain_vec.astype(jnp.float32)).astype(jnp.bfloat16)


def rope_tables(ctx_len, head_dim):
    inv_freq = ROPE_THETA ** (-2.0 * jnp.arange(head_dim // 2, dtype=jnp.float32) / head_dim)
    angles = ctx_len.astype(jnp.float32)[:, None] * inv_freq[None, :]
    return jnp.cos(angles), jnp.sin(angles)


def rotary(vectors, cos_t, sin_t):
    half_dim = vectors.shape[-1] // 2
    first_half = vectors[..., :half_dim]
    second_half = vectors[..., half_dim:]
    return jnp.concatenate([first_half * cos_t - second_half * sin_t, second_half * cos_t + first_half * sin_t], axis=-1)


def mlp_part(hidden, g_mlp, w_gate, w_up, w_down):
    normed = rms_norm(hidden, g_mlp)
    gate_pre = jnp.dot(normed, w_gate, preferred_element_type=jnp.float32)
    up_proj = jnp.dot(normed, w_up, preferred_element_type=jnp.float32)
    act_out = (jax.nn.silu(gate_pre) * up_proj).astype(jnp.bfloat16)
    return jnp.dot(act_out, w_down, preferred_element_type=jnp.float32)


def local_attention(x_in, ctx_len, g_attn, w_qkv, k_cache, v_cache, kvp_index):
    batch_rows, block_len, kv_local, head_dim = k_cache.shape
    group_size = w_qkv.shape[1] // (kv_local * head_dim) - 2
    normed = rms_norm(x_in, g_attn)
    qkv_all = jnp.dot(normed, w_qkv, preferred_element_type=jnp.float32).reshape(batch_rows, kv_local, group_size + 2, head_dim)
    cos_t, sin_t = rope_tables(ctx_len, head_dim)
    queries = rotary(qkv_all[:, :, :group_size], cos_t[:, None, None, :], sin_t[:, None, None, :]).astype(jnp.bfloat16)
    key_new = rotary(qkv_all[:, :, group_size], cos_t[:, None, :], sin_t[:, None, :]).astype(jnp.bfloat16)
    val_new = qkv_all[:, :, group_size + 1].astype(jnp.bfloat16)
    positions = kvp_index * block_len + jnp.arange(block_len)
    hit_mask = (positions[None, :] == ctx_len[:, None])[:, :, None, None]
    k_out = jnp.where(hit_mask, key_new[:, None], k_cache)
    v_out = jnp.where(hit_mask, val_new[:, None], v_cache)
    scores = jnp.einsum("bgrd,btgd->bgrt", queries, k_out, preferred_element_type=jnp.float32) * head_dim ** -0.5
    valid = (positions[None, :] <= ctx_len[:, None])[:, None, None, :]
    scores = jnp.where(valid, scores, NEG_FILL)
    local_max = jnp.max(scores, axis=-1)
    prob_w = jnp.exp(scores - local_max[..., None])
    local_sum = jnp.sum(prob_w, axis=-1)
    local_acc = jnp.einsum("bgrt,btgd->bgrd", prob_w.astype(jnp.bfloat16), v_out, preferred_element_type=jnp.float32)
    return local_max, local_sum, local_acc, k_out, v_out


def solution(mesh):
    x_spec = P("dp", None)
    cache_spec = P("dp", "kvp", "tp", None)
    model_axes = ("tp", "kvp")

    def layer_step(x_in, ctx_len, g_attn, g_mlp, w_qkv, w_o, w_gate, w_up, w_down, k_cache, v_cache):
        kvp_index = lax.axis_index("kvp")
        local_max, local_sum, local_acc, k_out, v_out = local_attention(x_in, ctx_len, g_attn, w_qkv, k_cache, v_cache, kvp_index)
        batch_rows = local_acc.shape[0]
        attn_width = local_acc.shape[1] * local_acc.shape[2] * local_acc.shape[3]
        rows_own = w_o.shape[0]
        global_max = lax.pmax(local_max, "kvp")
        rescale = jnp.exp(local_max - global_max)
        denom_sum = lax.psum(local_sum * rescale, "kvp")
        acc_part = (local_acc * rescale[..., None]).reshape(batch_rows, attn_width)
        acc_own = lax.psum_scatter(acc_part, "kvp", scatter_dimension=1, tiled=True)
        denom_rows = jnp.broadcast_to(denom_sum[..., None], local_acc.shape).reshape(batch_rows, attn_width)
        denom_own = lax.dynamic_slice_in_dim(denom_rows, kvp_index * rows_own, rows_own, axis=1)
        attn_own = (acc_own / denom_own).astype(jnp.bfloat16)
        attn_sum = lax.psum(jnp.dot(attn_own, w_o, preferred_element_type=jnp.float32), model_axes)
        hidden = (x_in.astype(jnp.float32) + attn_sum).astype(jnp.bfloat16)
        mlp_sum = lax.psum(mlp_part(hidden, g_mlp, w_gate, w_up, w_down), model_axes)
        x_out = (hidden.astype(jnp.float32) + mlp_sum).astype(jnp.bfloat16)
        return x_out, k_out, v_out

    in_specs = (x_spec, P("dp"), P(None), P(None), P(None, "tp"), P(model_axes, None), P(None, model_axes), P(None, model_axes), P(model_axes, None), cache_spec, cache_spec)
    return jax.shard_map(layer_step, mesh=mesh, in_specs=in_specs, out_specs=(x_spec, cache_spec, cache_spec), check_vma=False)
```

profile of v0, /device:TPU:0, one launch (start us, length us, event | category | flops | bytes accessed | tf_op | source)
XLA Modules:
  0.0 310.6 jit_solution(4574426536904766289)
XLA Ops:
  7.2 1.3 fusion.14
  8.5 0.7 convert_element_type.53
  9.3 10.4 %fusion.25 = f32[32,1792]{1,0:T(8,128)} fusion(bf16[5120,1792]{1,0:T(8,128)(2,1)} %param.15, bf16[32,5120]{1,0:T(8,128)(2,1)} %param.11, f32[5120]{0:T(1024)S(1)} %convert_element_type.53, f32[32]{0:T(128)S(1)} %add_rsqrt_fusion.1), kind=kOutput, calls=%fused_computation.29 | convolution fusion | flops 587857920 | bytes 18927744 | tf_op jit(solution)/shard_map/dot_general | solution.py:42
  19.6 1.0 reshape.203
  20.6 0.7 slice.30
  21.3 0.7 slice.43
  22.0 0.1 multiply_cosine_fusion
  22.2 0.2 subtract_convert_fusion
  22.4 0.9 subtract_convert_fusion.1
  23.3 0.8 copy.40
  24.1 0.1 pad_maximum_fusion
  24.2 13.6 %broadcast_select_fusion.1 = (bf16[32,256,2,128]{3,2,1,0:T(2,128)(2,1)S(1)}, bf16[32,256,2,128]{3,2,1,0:T(2,128)(2,1)}) fusion(bf16[32,256,2,128]{3,2,1,0:T(2,128)(2,1)} %param.20, pred[32,256]{1,0:T(8,128)(4,1)S(1)} %get-tuple-element.14, bf16[32,2,128]{2,1,0:T(2,128)(2,1)S(1)} %pad_maximum_fusion, bf16[32,256,2,128]{3,2,1,0:T(2,128)(2,1)} %param.21, ...), kind=kLoop, calls=%fused_computation.1 | loop fusion | flops 4194304 | bytes 16818176 | tf_op jit(solution)/shard_map/jit(_where)/select_n | solution.py:49
  37.8 2.0 copy-done.2
  39.8 2.0 fusion.50
  41.9 13.0 %pmax.7 = f32[32,2,5]{2,1,0:T(2,128)S(1)} all-reduce(f32[32,2,5]{2,1,0:T(2,128)S(1)} %get-tuple-element.17), channel_id=1, replica_groups=mesh['dp'=2,'tp'=4,'kvp'=4] {'kvp'}, use_global_device_ids=true, to_apply=%region_2.3 | all-reduce | flops 320 | bytes 2560 | tf_op jit(solution)/shard_map/pmax | solution.py:72
  54.9 1.3 fusion.23
  56.2 3.8 %fusion.11 = f32[32,2,5,128]{3,2,1,0:T(8,128)} fusion(bf16[32,256,2,128]{3,2,1,0:T(2,128)(2,1)} %get-tuple-element.12, f32[32,2,5,256]{3,2,1,0:T(8,128)} %get-tuple-element.18, f32[32,2,5]{2,1,0:T(2,128)S(1)} %get-tuple-element.17, f32[32,2,5]{2,1,0:T(2,128)S(1)} %bitcast.26), kind=kOutput, calls=%fused_computation.10 | convolution fusion | flops 21176320 | bytes 4688384 | tf_op jit(solution)/shard_map/bgrt,btgd->bgrd/dot_general | solution.py:57
  60.0 2.0 copy.26
  62.1 10.9 %psum.21 = f32[32,2,5]{2,1,0:T(2,128)} all-reduce(f32[32,2,5]{2,1,0:T(2,128)S(1)} %bitcast.23), channel_id=1, replica_groups=mesh['dp'=2,'tp'=4,'kvp'=4] {'kvp'}, use_global_device_ids=true, to_apply=%region_5.6 | all-reduce | flops 320 | bytes 2560 | tf_op jit(solution)/shard_map/psum | solution.py:74
  73.0 0.9 broadcast_in_dim.43
  73.8 0.7 reshape.205
  74.6 10.2 %reduce-scatter.4.cloned.1.call-done = f32[320,32]{1,0:T(8,128)} async-done(((f32[1280,32]{1,0:T(8,128)}), f32[320,32]{1,0:T(8,128)}) %reduce-scatter.4.cloned.1.call-update) | async-done | bytes 40976
  84.8 1.0 copy.25
  85.8 2.4 fusion.44
  88.3 0.2 all-reduce.5.cloned.1.call-start
  88.5 92.0 %all-reduce.3.cloned.1.call-done = f32[32,5120]{1,0:T(8,128)} async-done(((f32[32,5120]{1,0:T(8,128)}), f32[32,5120]{1,0:T(8,128)}) %all-reduce.3.cloned.1.call-update) | async-done | bytes 655376 | tf_op jit(solution)/shard_map/psum | solution.py:80
  180.5 1.4 fusion.18
  181.9 0.7 copy-done.3
  182.6 11.2 %fusion.42 = f32[32,1728]{1,0:T(8,128)S(1)} fusion(bf16[5120,1728]{0,1:T(8,128)(2,1)} %param.17, bf16[32,5120]{1,0:T(8,128)(2,1)S(1)} %get-tuple-element.4, f32[5120]{0:T(1024)S(1)} %convert_element_type.61, f32[32]{0:T(128)S(1)} %add_rsqrt_fusion), kind=kOutput, calls=%fused_computation.44 | convolution fusion | flops 566886400 | bytes 18264192 | tf_op jit(solution)/shard_map/dot_general | solution.py:32
  193.9 16.9 %fusion.22 = f32[32,5120]{1,0:T(8,128)} fusion(bf16[1728,5120]{1,0:T(8,128)(2,1)} %param.19, bf16[5120,1728]{0,1:T(8,128)(2,1)} %param.18, f32[32,1728]{1,0:T(8,128)S(1)} %fusion.42, bf16[32,5120]{1,0:T(8,128)(2,1)} %copy-done.3, f32[5120]{0:T(1024)S(1)} %convert_element_type.61, f32[32]{0:T(128)S(1)} %add_rsqrt_fusion), kind=kOutput, calls=%fused_computation.25 | convolution fusion | flops 1133449216 | bytes 36614272 | tf_op jit(solution)/shard_map/dot_general | solution.py:35
  210.8 91.3 %all-reduce.5.cloned.1.call-done = f32[32,5120]{1,0:T(8,128)} async-done(((f32[32,5120]{1,0:T(8,128)}), f32[32,5120]{1,0:T(8,128)}) %all-reduce.5.cloned.1.call-update) | async-done | bytes 655376 | tf_op jit(solution)/shard_map/psum | solution.py:82
  302.1 1.9 fusion.21
  (24 shorter events, 0.3 us)
Async XLA Ops:
  7.2 78.6 %copy-start = (bf16[320,5120]{1,0:T(8,128)(2,1)S(1)}, bf16[320,5120]{1,0:T(8,128)(2,1)}, u32[]{:S(2)}) copy-start(bf16[320,5120]{1,0:T(8,128)(2,1)} %param.16) | copy-start | bytes 9830404
  7.2 77.6 %reduce-scatter.4.cloned.1.call-start = ((), (), s32[]{:S(2)}) async-start(), calls=%async_computation.3 | async-start | bytes 819200
  9.3 12.7 %copy-start.5 = (s32[32]{0:T(128)S(1)}, s32[32]{0:T(128)}, u32[]{:S(2)}) copy-start(s32[32]{0:T(128)} %param.12) | copy-start | bytes 388
  37.8 2.0 copy-start.2
  60.0 28.5 %copy-start.4 = (bf16[5120]{0:T(1024)(128)(2,1)S(1)}, bf16[5120]{0:T(1024)(128)(2,1)}, u32[]{:S(2)}) copy-start(bf16[5120]{0:T(1024)(128)(2,1)} %param.14) | copy-start | bytes 30724
  62.0 118.5 %all-reduce.3.cloned.1.call-start = ((), (), s32[]{:S(2)}) async-start(), calls=%async_computation.1 | async-start | bytes 1310720 | tf_op jit(solution)/shard_map/psum | solution.py:80
  88.3 213.8 %all-reduce.5.cloned.1.call-start = ((), (), s32[]{:S(2)}) async-start(), calls=%async_computation.2 | async-start | bytes 1310720 | tf_op jit(solution)/shard_map/psum | solution.py:82
  181.9 0.7 copy-start.3
  193.8 110.2 %copy-start.1 = (bf16[320,5120]{1,0:T(8,128)(2,1)S(1)}, bf16[320,5120]{1,0:T(8,128)(2,1)}, u32[]{:S(2)}) copy-start(bf16[320,5120]{1,0:T(8,128)(2,1)} %param.16) | copy-start | bytes 9830404
Sparse Core Ops, SparseCore 0:
  62.2 22.5 reduce-scatter.3
  88.4 92.1 all-reduce.2
  210.9 91.1 all-reduce.4
where the time goes:
time: 311 us
  waiting for transfers between devices  194 us (62%)
  matrix products  46.7 us (15%)
  blocking collectives  23.8 us (8%)
  other arithmetic  21.8 us (7%)
  between operations  13.9 us (4%)
  local copies, waits for them, and re-layouts  10.5 us (3%)
    psum x1, waiting for transfers between devices, layer_step(): lax.psum(jnp.dot(attn_own, w_o, preferred_element_type=jnp.float32), mode...  92 us
    psum x1, waiting for transfers between devices, layer_step(): lax.psum(mlp_part(hidden, g_mlp, w_gate, w_up, w_down), model_axes)  91.3 us
    dot_general x1, matrix products, mlp_part(): return jnp.dot(act_out, w_down, preferred_element_type=jnp.float32)  16.9 us
    select_n x1, other arithmetic, local_attention(): k_out = jnp.where(hit_mask, key_new[:, None], k_cache)  13.6 us
    pmax x1, blocking collectives, layer_step(): global_max = lax.pmax(local_max, 'kvp')  13 us
    dot_general x1, matrix products, mlp_part(): gate_pre = jnp.dot(normed, w_gate, preferred_element_type=jnp.float32)  11.2 us
    psum x1, blocking collectives, layer_step(): denom_sum = lax.psum(local_sum * rescale, 'kvp')  10.9 us
    dot_general x1, matrix products, local_attention(): jnp.dot(normed, w_qkv, preferred_element_type=jnp.float32)  10.4 us
  transfers between devices with their start and end apart: 3, of which 3 were waited for; matrix products, arithmetic and copies ran while one was open for 1% of the time, Pallas kernels for 0%

commit v1 on v0

v1 whole, which is shorter than its diff:
```python
import functools

import jax
import jax.numpy as jnp
from jax import lax
from jax.experimental import pallas as pl
from jax.experimental.pallas import tpu as pltpu
from jax.sharding import PartitionSpec as P

ROPE_THETA = 500000.0
EPS = 1e-5
NEG_FILL = -1e30
LANES = 128
HALF = 16
MESH = pl.DeviceIdType.MESH
QKV_STEPS = 10
KV_STEPS = 4
CHUNKS = 5
UNITS = 8
F32 = jnp.float32
BF16 = jnp.bfloat16


def rope_rows(ctx_len, head_dim):
    inv_freq = ROPE_THETA ** (-2.0 * jnp.arange(head_dim // 2, dtype=F32) / head_dim)
    angles = ctx_len.astype(F32)[:, None] * inv_freq[None, :]
    cos_t, sin_t = jnp.cos(angles), jnp.sin(angles)
    return jnp.concatenate([cos_t, cos_t], axis=-1), jnp.concatenate([-sin_t, sin_t], axis=-1)


def attention_kernel(
    ctx_ref, x_ref, g_ref, cos_ref, sin_ref, w_hbm, k_hbm, v_hbm,
    acc_ref, ml_ref, k_out, v_out,
    w_buf, k_buf, v_buf, n_buf, c_buf, q_buf, kn_buf, vn_buf, m_buf, l_buf,
    w_sem, k_sem, v_sem, ko_sem, vo_sem,
):
    batch, width = x_ref.shape
    rows_w = width // QKV_STEPS
    rows_kv = batch // KV_STEPS
    block2 = k_buf.shape[1]
    block = block2 // 2
    heads = c_buf.shape[1] // LANES
    group = heads // 2 - 2

    def w_copy(i):
        rows = pl.ds(i * rows_w, rows_w)
        return pltpu.make_async_copy(w_hbm.at[rows, :], w_buf.at[rows, :], w_sem.at[i])

    def kv_copy(i, src, dst, sem):
        rows = pl.ds(i * rows_kv, rows_kv)
        return pltpu.make_async_copy(src.at[rows], dst.at[rows], sem.at[i])

    for i in range(QKV_STEPS):
        w_copy(i).start()
    for i in range(KV_STEPS):
        kv_copy(i, k_hbm, k_buf, k_sem).start()
        kv_copy(i, v_hbm, v_buf, v_sem).start()

    sq = jnp.zeros((batch, LANES), F32)
    for c in range(width // LANES):
        xb = x_ref[:, c * LANES:(c + 1) * LANES].astype(F32)
        sq = sq + xb * xb
    inv = lax.rsqrt(jnp.sum(sq, axis=-1, keepdims=True) / width + EPS)
    for i in range(QKV_STEPS):
        cols = slice(i * rows_w, (i + 1) * rows_w)
        xb = x_ref[:, cols].astype(F32)
        n_buf[i] = (xb * inv * g_ref[:, cols].astype(F32)).astype(BF16)

    c_buf[...] = jnp.zeros_like(c_buf)

    def qkv_step(i, carry):
        w_copy(i).wait()
        rows = pl.ds(pl.multiple_of(i * rows_w, rows_w), rows_w)
        c_buf[...] += jnp.dot(n_buf[i], w_buf[rows, :], preferred_element_type=F32)
        return carry

    lax.fori_loop(0, QKV_STEPS, qkv_step, 0)

    cos_t, sin_t = cos_ref[...], sin_ref[...]

    def rotary(v):
        return v * cos_t + pltpu.roll(v, LANES // 2, 1) * sin_t

    q_buf[...] = jnp.zeros_like(q_buf)
    for g in range(2):
        base = g * (group + 2)
        for r in range(group):
            v = c_buf[:, (base + r) * LANES:(base + r + 1) * LANES]
            h = g * group + r
            q_buf[h * batch:(h + 1) * batch, :] = rotary(v).astype(BF16).astype(F32)
        v = c_buf[:, (base + group) * LANES:(base + group + 1) * LANES]
        kn_buf[g * batch:(g + 1) * batch, :] = rotary(v).astype(BF16).astype(F32)
        v = c_buf[:, (base + group + 1) * LANES:(base + group + 2) * LANES]
        vn_buf[g * batch:(g + 1) * batch, :] = v.astype(BF16).astype(F32)

    off = lax.axis_index("kvp") * block
    scale = LANES ** -0.5
    col = lax.broadcasted_iota(jnp.int32, (16, block2), 1)
    row = lax.broadcasted_iota(jnp.int32, (16, block2), 0)
    own = (col & 1) == (row >= group).astype(jnp.int32)
    pos = jnp.where(own, col >> 1, 1 << 20)
    trow = lax.broadcasted_iota(jnp.int32, (16, LANES), 0)
    lane = lax.broadcasted_iota(jnp.int32, (16, LANES), 1)
    m_buf[...] = jnp.zeros_like(m_buf)
    l_buf[...] = jnp.zeros_like(l_buf)

    def kv_step(i, carry):
        kv_copy(i, k_hbm, k_buf, k_sem).wait()
        kv_copy(i, v_hbm, v_buf, v_sem).wait()
        for u in range(rows_kv):
            b = i * rows_kv + u
            rel = ctx_ref[b] - off
            hit = jnp.logical_and(rel >= 0, rel < block)
            relc = jnp.where(hit, rel, 0)
            first = pl.multiple_of((relc >> 3) * 16, 16)
            sel = (trow >> 1) == jnp.where(hit, relc & 7, 64)
            for buf, new in ((k_buf, kn_buf), (v_buf, vn_buf)):
                new0 = new[pl.ds(b, 1), :]
                new1 = new[pl.ds(batch + b, 1), :]
                tile = buf[b, pl.ds(first, 16), :].astype(F32)
                fresh = jnp.where((trow & 1) == 0, new0, new1)
                buf[b, pl.ds(first, 16), :] = jnp.where(sel, fresh, tile).astype(BF16)
        kv_copy(i, k_buf, k_out, ko_sem).start()
        kv_copy(i, v_buf, v_out, vo_sem).start()
        for u in range(rows_kv):
            b = i * rows_kv + u
            rel = ctx_ref[b] - off
            q = q_buf[pl.ds(b, 16, stride=batch), :].astype(BF16)
            s = lax.dot_general(q, k_buf[b], (((1,), (1,)), ((), ())), preferred_element_type=F32) * scale
            s = jnp.where(pos <= rel, s, NEG_FILL)
            m = jnp.max(s, axis=-1, keepdims=True)
            w = jnp.exp(s - m)
            l = jnp.sum(w, axis=-1, keepdims=True)
            acc_ref[pl.ds(b, 16, stride=batch), :] = jnp.dot(w.astype(BF16), v_buf[b], preferred_element_type=F32)
            m_buf[...] += jnp.where(lane == b, m, 0.0)
            l_buf[...] += jnp.where(lane == b, l, 0.0)
        return carry

    lax.fori_loop(0, KV_STEPS, kv_step, 0)
    stats = jnp.concatenate([m_buf[...], l_buf[...], jnp.zeros((LANES - 32, LANES), F32)], axis=0)
    ml_ref[...] = stats.T[:batch, :]
    for i in range(KV_STEPS):
        kv_copy(i, k_buf, k_out, ko_sem).wait()
        kv_copy(i, v_buf, v_out, vo_sem).wait()


def tail_kernel(
    acc_ref, ml_ref, x_ref, g_ref, wo_hbm, wg_hbm, wu_hbm, wd_hbm,
    out_ref,
    wo_buf, wg_buf, wu_buf, wd_buf, racc, rml, a_buf, part, rc_buf, ry_buf, rz_buf, full, h_buf, n_buf, act,
    wo_sem, wg_sem, wu_sem, wd_sem, sa_sem, ra_sem, sm_sem, rm_sem, sc_sem, rc_sem, sy_sem, ry_sem, sz_sem, rz_sem,
):
    batch, width = x_ref.shape
    ff = act.shape[1]
    tp = lax.axis_index("tp")
    kvp = lax.axis_index("kvp")
    y = kvp // 2
    core = kvp % 2
    odd = core
    kv_peers = (y * 2 + (1 - core), (1 - y) * 2 + core, (1 - y) * 2 + (1 - core))
    z_peers = tuple((tp + d) % 4 for d in (1, 2, 3))

    barrier = pltpu.get_barrier_semaphore()
    for peer in kv_peers:
        pl.semaphore_signal(barrier, inc=1, device_id={"kvp": peer}, device_id_type=MESH)
    for peer in z_peers:
        pl.semaphore_signal(barrier, inc=1, device_id={"tp": peer}, device_id_type=MESH)

    rows_o = wo_hbm.shape[0]
    first = pl.multiple_of(odd * 64, 64)
    wo_copy = pltpu.make_async_copy(wo_hbm, wo_buf.at[pl.ds(first, rows_o), :], wo_sem)
    wo_copy.start()
    gap = pl.multiple_of((1 - odd) * rows_o, 64)
    wo_buf[pl.ds(gap, 64), :] = jnp.zeros((64, width), BF16)

    def stream(src, dst, sem, pieces):
        step = src.shape[0] // pieces
        for i in range(pieces):
            rows = pl.ds(i * step, step)
            pltpu.make_async_copy(src.at[rows, :], dst.at[rows, :], sem).start()

    stream(wg_hbm, wg_buf, wg_sem, 8)
    stream(wu_hbm, wu_buf, wu_sem, 8)
    stream(wd_hbm, wd_buf, wd_sem, 9)

    pl.semaphore_wait(barrier, 6)

    sends = []
    for d, peer in enumerate(kv_peers):
        head0 = (5 * peer) // 2
        for src, dst, ss, rs in (
            (acc_ref.at[pl.ds(head0, 3)], racc.at[d], sa_sem, ra_sem),
            (ml_ref, rml.at[d], sm_sem, rm_sem),
        ):
            copy = pltpu.make_async_remote_copy(
                src, dst, ss.at[d], rs.at[d], device_id={"kvp": peer}, device_id_type=MESH
            )
            copy.start()
            sends.append(copy)
    for copy in sends:
        copy.wait_recv()
    head0 = (5 * kvp) // 2
    lane = lax.broadcasted_iota(jnp.int32, (batch, LANES), 1)
    stats = [ml_ref[...]] + [rml[d] for d in range(3)]
    for i in range(3):
        ms = [jnp.sum(jnp.where(lane == head0 + i, st, 0.0), axis=-1, keepdims=True) for st in stats]
        ls = [jnp.sum(jnp.where(lane == head0 + i + 16, st, 0.0), axis=-1, keepdims=True) for st in stats]
        top = functools.reduce(jnp.maximum, ms)
        ws = [jnp.exp(m - top) for m in ms]
        denom = functools.reduce(jnp.add, [l * w for l, w in zip(ls, ws)])
        accs = [acc_ref[head0 + i]] + [racc[d, i] for d in range(3)]
        numer = functools.reduce(jnp.add, [a * w for a, w in zip(accs, ws)])
        a_buf[:, i * LANES:(i + 1) * LANES] = (numer / denom).astype(BF16)

    def remote(src, dst, ss, rs, device):
        copy = pltpu.make_async_remote_copy(src, dst, ss, rs, device_id=device, device_id_type=MESH)
        copy.start()
        return copy

    core_dev = {"kvp": kv_peers[0]}
    y_dev = {"kvp": kv_peers[1]}

    def all_reduce(ar, produce):
        cs, ys, zs, started = [], [], [], []
        for j in range(CHUNKS):
            produce(j)
            cs.append(remote(part.at[1 - core, j], rc_buf.at[ar, j], sc_sem.at[ar, 0, j], rc_sem.at[ar, 0, j], core_dev))
        for j in range(CHUNKS):
            cs[j].wait_recv()
            part[core, j] += rc_buf[ar, j]
            ys.append(remote(part.at[core, j, pl.ds((1 - y) * 4, 4)], ry_buf.at[ar, j], sy_sem.at[ar, 0, j], ry_sem.at[ar, 0, j], y_dev))
        for j in range(CHUNKS):
            ys[j].wait_recv()
            part[core, j, pl.ds(y * 4, 4)] += ry_buf[ar, j]
            zs.append([
                remote(part.at[core, j, y * 4 + peer], rz_buf.at[ar, j, d], sz_sem.at[ar, 0, j, d], rz_sem.at[ar, 0, j, d], {"tp": peer})
                for d, peer in enumerate(z_peers)
            ])
        gz, gy, gc = [], [], []
        mine = y * 4 + tp
        for j in range(CHUNKS):
            total = part[core, j, mine]
            for d in range(3):
                zs[j][d].wait_recv()
                total = total + rz_buf[ar, j, d]
            full[ar, core, j, mine] = total
            gz.append([
                remote(full.at[ar, core, j, mine], full.at[ar, core, j, mine], sz_sem.at[ar, 1, j, d], rz_sem.at[ar, 1, j, d], {"tp": peer})
                for d, peer in enumerate(z_peers)
            ])
        for j in range(CHUNKS):
            for d in range(3):
                gz[j][d].wait_recv()
            block = full.at[ar, core, j, pl.ds(y * 4, 4)]
            gy.append(remote(block, block, sy_sem.at[ar, 1, j], ry_sem.at[ar, 1, j], y_dev))
        for j in range(CHUNKS):
            gy[j].wait_recv()
            block = full.at[ar, core, j]
            gc.append(remote(block, block, sc_sem.at[ar, 1, j], rc_sem.at[ar, 1, j], core_dev))
        for j in range(CHUNKS):
            gc[j].wait_recv()
        for copy in cs + ys + gy + gc:
            copy.wait_send()
        for copy in [c for group in zs + gz for c in group]:
            copy.wait_send()

    wo_copy.wait()

    def store_part(j, half, res):
        for r in range(2):
            for u in range(res.shape[1] // LANES):
                part[r, j, half + u] = res[r * HALF:(r + 1) * HALF, u * LANES:(u + 1) * LANES]

    def produce_o(j):
        cols = slice(j * UNITS * LANES, (j + 1) * UNITS * LANES)
        store_part(j, 0, jnp.dot(a_buf[...], wo_buf[:, cols], preferred_element_type=F32))

    all_reduce(0, produce_o)

    sq = [jnp.zeros((HALF, LANES), F32) for _ in range(2)]
    for c in range(width // LANES):
        j, u = divmod(c, UNITS)
        for r in range(2):
            rows, cols = slice(r * HALF, (r + 1) * HALF), slice(c * LANES, (c + 1) * LANES)
            h = (x_ref[rows, cols].astype(F32) + full[0, r, j, u]).astype(BF16)
            h_buf[rows, cols] = h
            hf = h.astype(F32)
            sq[r] = sq[r] + hf * hf
    for r in range(2):
        rows = slice(r * HALF, (r + 1) * HALF)
        inv = lax.rsqrt(jnp.sum(sq[r], axis=-1, keepdims=True) / width + EPS)
        for c in range(width // LANES):
            cols = slice(c * LANES, (c + 1) * LANES)
            n_buf[rows, cols] = (h_buf[rows, cols].astype(F32) * inv * g_ref[:, cols].astype(F32)).astype(BF16)

    pltpu.make_async_copy(wg_hbm, wg_buf, wg_sem).wait()
    pltpu.make_async_copy(wu_hbm, wu_buf, wu_sem).wait()

    def mlp_tile(cols):
        gate = jnp.dot(n_buf[...], wg_buf[:, cols], preferred_element_type=F32)
        up = jnp.dot(n_buf[...], wu_buf[:, cols], preferred_element_type=F32)
        act[:, cols] = (jax.nn.silu(gate) * up).astype(BF16)

    tiles = ff // 256

    def mlp_step(i, carry):
        mlp_tile(pl.ds(pl.multiple_of(i * 256, 256), 256))
        return carry

    lax.fori_loop(0, tiles, mlp_step, 0)
    if ff % 256:
        mlp_tile(slice(tiles * 256, ff))

    pltpu.make_async_copy(wd_hbm, wd_buf, wd_sem).wait()

    def produce_down(j):
        for half in range(2):
            cols = slice((2 * j + half) * 512, (2 * j + half + 1) * 512)
            store_part(j, half * 4, jnp.dot(act[...], wd_buf[:, cols], preferred_element_type=F32))

    all_reduce(1, produce_down)

    for c in range(width // LANES):
        j, u = divmod(c, UNITS)
        for r in range(2):
            rows, cols = slice(r * HALF, (r + 1) * HALF), slice(c * LANES, (c + 1) * LANES)
            out_ref[rows, cols] = (h_buf[rows, cols].astype(F32) + full[1, r, j, u]).astype(BF16)
    for copy in sends:
        copy.wait_send()


def vmem():
    return pl.BlockSpec(memory_space=pltpu.VMEM)


def anywhere():
    return pl.BlockSpec(memory_space=pl.ANY)


def attention_call(x_in, ctx_len, g_attn, w_qkv, k_cache, v_cache):
    batch, width = x_in.shape
    block, kv_local, head_dim = k_cache.shape[1:]
    cols = w_qkv.shape[1]
    cos_t, sin_t = rope_rows(ctx_len, head_dim)
    flat = (batch, block * kv_local, head_dim)
    dma = pltpu.SemaphoreType.DMA
    acc, ml, k_out, v_out = pl.pallas_call(
        attention_kernel,
        name="attention",
        out_shape=(
            jax.ShapeDtypeStruct((16 * batch, head_dim), F32),
            jax.ShapeDtypeStruct((batch, LANES), F32),
            jax.ShapeDtypeStruct(flat, BF16),
            jax.ShapeDtypeStruct(flat, BF16),
        ),
        in_specs=[pl.BlockSpec(memory_space=pltpu.SMEM)] + [vmem()] * 4 + [anywhere()] * 3,
        out_specs=(vmem(), vmem(), anywhere(), anywhere()),
        scratch_shapes=[
            pltpu.VMEM((width, cols), BF16),
            pltpu.VMEM(flat, BF16),
            pltpu.VMEM(flat, BF16),
            pltpu.VMEM((QKV_STEPS, batch, width // QKV_STEPS), BF16),
            pltpu.VMEM((batch, cols), F32),
            pltpu.VMEM((16 * batch, head_dim), F32),
            pltpu.VMEM((2 * batch, head_dim), F32),
            pltpu.VMEM((2 * batch, head_dim), F32),
            pltpu.VMEM((16, LANES), F32),
            pltpu.VMEM((16, LANES), F32),
            dma((QKV_STEPS,)),
            dma((KV_STEPS,)),
            dma((KV_STEPS,)),
            dma((KV_STEPS,)),
            dma((KV_STEPS,)),
        ],
        compiler_params=pltpu.CompilerParams(vmem_limit_bytes=60 * 1024 * 1024),
        cost_estimate=pl.CostEstimate(flops=2 * batch * width * cols, bytes_accessed=36 << 20, transcendentals=1 << 19),
    )(ctx_len, x_in, g_attn.reshape(1, width), cos_t, sin_t, w_qkv, k_cache.reshape(flat), v_cache.reshape(flat))
    return acc.reshape(16, batch, head_dim), ml, k_out.reshape(k_cache.shape), v_out.reshape(v_cache.shape)


def tail_call(acc, ml, x_in, g_mlp, w_o, w_gate, w_up, w_down):
    batch, width = x_in.shape
    ff = w_gate.shape[1]
    dma = pltpu.SemaphoreType.DMA
    unit = (HALF, LANES)
    return pl.pallas_call(
        tail_kernel,
        name="tail",
        out_shape=jax.ShapeDtypeStruct((batch, width), BF16),
        in_specs=[vmem()] * 4 + [anywhere()] * 4,
        out_specs=vmem(),
        scratch_shapes=[
            pltpu.VMEM((w_o.shape[0] + 64, width), BF16),
            pltpu.VMEM((width, ff), BF16),
            pltpu.VMEM((width, ff), BF16),
            pltpu.VMEM((ff, width), BF16),
            pltpu.VMEM((3, 3, batch, LANES), F32),
            pltpu.VMEM((3, batch, LANES), F32),
            pltpu.VMEM((batch, 3 * LANES), BF16),
            pltpu.VMEM((2, CHUNKS, UNITS) + unit, F32),
            pltpu.VMEM((2, CHUNKS, UNITS) + unit, F32),
            pltpu.VMEM((2, CHUNKS, 4) + unit, F32),
            pltpu.VMEM((2, CHUNKS, 3) + unit, F32),
            pltpu.VMEM((2, 2, CHUNKS, UNITS) + unit, F32),
            pltpu.VMEM((batch, width), BF16),
            pltpu.VMEM((batch, width), BF16),
            pltpu.VMEM((batch, ff), BF16),
            dma(()), dma(()), dma(()), dma(()),
            dma((3,)), dma((3,)), dma((3,)), dma((3,)),
            dma((2, 2, CHUNKS)), dma((2, 2, CHUNKS)),
            dma((2, 2, CHUNKS)), dma((2, 2, CHUNKS)),
            dma((2, 2, CHUNKS, 3)), dma((2, 2, CHUNKS, 3)),
        ],
        compiler_params=pltpu.CompilerParams(
            collective_id=0, has_side_effects=True, vmem_limit_bytes=67_043_328
        ),
        cost_estimate=pl.CostEstimate(flops=6 * batch * width * ff, bytes_accessed=58 << 20, transcendentals=1 << 17),
    )(acc, ml, x_in, g_mlp.reshape(1, width), w_o, w_gate, w_up, w_down)


def solution(mesh):
    x_spec = P("dp", None)
    cache_spec = P("dp", "kvp", "tp", None)
    model_axes = ("tp", "kvp")

    def layer_step(x_in, ctx_len, g_attn, g_mlp, w_qkv, w_o, w_gate, w_up, w_down, k_cache, v_cache):
        acc, ml, k_out, v_out = attention_call(x_in, ctx_len, g_attn, w_qkv, k_cache, v_cache)
        x_out = tail_call(acc, ml, x_in, g_mlp, w_o, w_gate, w_up, w_down)
        return x_out, k_out, v_out

    in_specs = (x_spec, P("dp"), P(None), P(None), P(None, "tp"), P(model_axes, None), P(None, model_axes), P(None, model_axes), P(model_axes, None), cache_spec, cache_spec)
    return jax.shard_map(layer_step, mesh=mesh, in_specs=in_specs, out_specs=(x_spec, cache_spec, cache_spec), check_vma=False)
```

time: 311 us -> 142 us (0.46)
  waiting for transfers between devices: 194 us -> 0 us
  Pallas kernels: 0 us -> 87.9 us
  matrix products: 46.7 us -> 0 us
  local copies, waits for them, and re-layouts: 10.5 us -> 50.3 us
  blocking collectives: 23.8 us -> 0 us
  other arithmetic: 21.8 us -> 1.5 us
  between operations: 13.9 us -> 0.65 us
    psum x2 -> x0, waiting for transfers between devices: 183 us -> none  [the longest x1 92 us: layer_step(): lax.psum(jnp.dot(attn_own, w_o, preferred_element_type=jnp.float32), mode...]
    pallas_call x0 -> x2, Pallas kernels: none -> 87.9 us  [the longest x1 67.9 us: tail_call(): pl.pallas_call(tail_kernel, name='tail', out_shape=jax.ShapeDtypeStruct((...]
    dot_general x6 -> x0, matrix products: 46.7 us -> none  [the longest x1 16.9 us: mlp_part(): return jnp.dot(act_out, w_down, preferred_element_type=jnp.float32)]
    unnamed x14 -> x3, local copies, waits for them, and re-layouts: 5.81 us -> 47.7 us
    select_n x1 -> x0, other arithmetic: 13.6 us -> none  [local_attention(): k_out = jnp.where(hit_mask, key_new[:, None], k_cache)]
    pmax x1 -> x0, blocking collectives: 13 us -> none  [layer_step(): global_max = lax.pmax(local_max, 'kvp')]
    psum x1 -> x0, blocking collectives: 10.9 us -> none  [layer_step(): denom_sum = lax.psum(local_sum * rescale, 'kvp')]
    unnamed x4 -> x0, waiting for transfers between devices: 10.3 us -> none
  transfers between devices with their start and end apart: 3 -> 0, of which waited for: 3 -> 0; matrix products, arithmetic and copies ran while one was open for 1% -> 0% of each run, Pallas kernels for 0% -> 0%
where the time goes in v1:
time: 142 us; the launch traced here: 140 us
  Pallas kernels  87.9 us (62%)
  local copies, waits for them, and re-layouts  50.3 us (35%)
  other arithmetic  1.5 us (1%)
    pallas_call x1, Pallas kernels, tail_call(): pl.pallas_call(tail_kernel, name='tail', out_shape=jax.ShapeDtypeStruct((...  67.9 us
    unnamed x3, local copies, waits for them, and re-layouts  47.7 us
    pallas_call x1, Pallas kernels, attention_call(): pl.pallas_call(attention_kernel, name='attention', out_shape=(jax.ShapeDt...  20 us

profile of v1, /device:TPU:0, one launch (start us, length us, event | category | flops | bytes accessed | tf_op | source)
XLA Modules:
  0.0 140.4 jit_solution(15482109208642054505)
XLA Ops:
  0.6 0.7 convert_element_type.3
  1.3 1.3 reshape.33.g_ref
  2.6 1.3 reshape.37.g_ref
  3.9 0.1 fusion
  4.1 0.7 pad_maximum_fusion
  4.8 20.0 %attention.1 = (f32[512,128]{1,0:T(8,128)}, f32[32,128]{1,0:T(8,128)}, bf16[32,512,128]{2,1,0:T(8,128)(2,1)}, bf16[32,512,128]{2,1,0:T(8,128)(2,1)}) custom-call(s32[32]{0:T(128)} %ctx_ref.1, bf16[32,5120]{1,0:T(8,128)(2,1)} %x_ref.3, bf16[1,5120]{1,0:T(2,128)(2,1)} %reshape.33.g_ref, f32[32,128]{1,0:T(8,128)} %get-tuple-element.14.cos_ref, ...), custom_call_target="tpu_custom_call" | custom-call | flops 587202560 | bytes 37748736 | tf_op jit(solution)/shard_map/attention/pallas_call | solution.py:347
  24.8 23.0 %copy.14.wg_hbm = bf16[5120,1728]{1,0:T(8,128)(2,1)} copy(bf16[5120,1728]{0,1:T(8,128)(2,1)} %param.17) | data formatting | bytes 35389440 | tf_op args[6]
  47.8 23.0 %copy.15.wu_hbm = bf16[5120,1728]{1,0:T(8,128)(2,1)} copy(bf16[5120,1728]{0,1:T(8,128)(2,1)} %param.18) | data formatting | bytes 35389440 | tf_op args[7]
  70.7 67.9 %tail.1 = bf16[32,5120]{1,0:T(8,128)(2,1)} custom-call(f32[16,32,128]{2,1,0:T(8,128)} %bitcast.7, f32[32,128]{1,0:T(8,128)} %get-tuple-element.8.ml_ref, bf16[32,5120]{1,0:T(8,128)(2,1)} %x_ref.3, bf16[1,5120]{1,0:T(2,128)(2,1)} %reshape.37.g_ref, bf16[320,5120]{1,0:T(8,128)(2,1)} %wo_hbm.1, bf16[5120,1728]{1,0:T(8,128)(2,1)} %copy.14.wg_hbm, ...), custom_call_target="tpu_custom_call" | custom-call | flops 1698693120 | bytes 60817408 | tf_op jit(solution)/shard_map/tail/pallas_call | solution.py:386
  138.7 1.7 %copy.17 = bf16[32,5120]{1,0:T(8,128)(2,1)} copy(bf16[32,5120]{1,0:T(8,128)(2,1)} %tail.1) | data formatting | bytes 655360
  (1 shorter events, 0.0 us)

commit v2 on v1

--- a/solution.py
+++ b/solution.py
@@ -16,22 +16,26 @@
 QKV_STEPS = 10
 KV_STEPS = 4
 CHUNKS = 5
+GROUPS = ((0, 3), (3, 5))
 UNITS = 8
 F32 = jnp.float32
 BF16 = jnp.bfloat16
 
 
 def rope_rows(ctx_len, head_dim):
-    inv_freq = ROPE_THETA ** (-2.0 * jnp.arange(head_dim // 2, dtype=F32) / head_dim)
-    angles = ctx_len.astype(F32)[:, None] * inv_freq[None, :]
-    cos_t, sin_t = jnp.cos(angles), jnp.sin(angles)
-    return jnp.concatenate([cos_t, cos_t], axis=-1), jnp.concatenate([-sin_t, sin_t], axis=-1)
+    half_dim = head_dim // 2
+    lane = jnp.arange(head_dim)
+    pair = (lane % half_dim).astype(F32)
+    inv_freq = ROPE_THETA ** (-2.0 * pair / head_dim)
+    angles = ctx_len[:, None].astype(F32) * inv_freq[None, :]
+    sign = jnp.where(lane < half_dim, -1.0, 1.0)
+    return jnp.cos(angles), jnp.sin(angles) * sign[None, :]
 
 
 def attention_kernel(
     ctx_ref, x_ref, g_ref, cos_ref, sin_ref, w_hbm, k_hbm, v_hbm,
     acc_ref, ml_ref, k_out, v_out,
-    w_buf, k_buf, v_buf, n_buf, c_buf, q_buf, kn_buf, vn_buf, m_buf, l_buf,
+    w_buf, k_buf, v_buf, n_buf, c_buf, q_buf, kn_buf, vn_buf,
     w_sem, k_sem, v_sem, ko_sem, vo_sem,
 ):
     batch, width = x_ref.shape
@@ -64,7 +68,7 @@
     for i in range(QKV_STEPS):
         cols = slice(i * rows_w, (i + 1) * rows_w)
         xb = x_ref[:, cols].astype(F32)
-        n_buf[i] = (xb * inv * g_ref[:, cols].astype(F32)).astype(BF16)
+        n_buf[i] = (xb * inv * g_ref[cols].astype(F32)[None, :]).astype(BF16)
 
     c_buf[...] = jnp.zeros_like(c_buf)
 
@@ -101,43 +105,50 @@
     pos = jnp.where(own, col >> 1, 1 << 20)
     trow = lax.broadcasted_iota(jnp.int32, (16, LANES), 0)
     lane = lax.broadcasted_iota(jnp.int32, (16, LANES), 1)
-    m_buf[...] = jnp.zeros_like(m_buf)
-    l_buf[...] = jnp.zeros_like(l_buf)
-
     def kv_step(i, carry):
+        m_all, l_all = carry
         kv_copy(i, k_hbm, k_buf, k_sem).wait()
         kv_copy(i, v_hbm, v_buf, v_sem).wait()
+        rels = [ctx_ref[i * rows_kv + u] - off for u in range(rows_kv)]
+        fresh = []
         for u in range(rows_kv):
             b = i * rows_kv + u
-            rel = ctx_ref[b] - off
-            hit = jnp.logical_and(rel >= 0, rel < block)
-            relc = jnp.where(hit, rel, 0)
+            hit = jnp.logical_and(rels[u] >= 0, rels[u] < block)
+            relc = jnp.where(hit, rels[u], 0)
             first = pl.multiple_of((relc >> 3) * 16, 16)
             sel = (trow >> 1) == jnp.where(hit, relc & 7, 64)
             for buf, new in ((k_buf, kn_buf), (v_buf, vn_buf)):
                 new0 = new[pl.ds(b, 1), :]
                 new1 = new[pl.ds(batch + b, 1), :]
                 tile = buf[b, pl.ds(first, 16), :].astype(F32)
-                fresh = jnp.where((trow & 1) == 0, new0, new1)
-                buf[b, pl.ds(first, 16), :] = jnp.where(sel, fresh, tile).astype(BF16)
+                row_pair = jnp.where((trow & 1) == 0, new0, new1)
+                fresh.append((buf, b, first, jnp.where(sel, row_pair, tile).astype(BF16)))
+        for buf, b, first, tile in fresh:
+            buf[b, pl.ds(first, 16), :] = tile
         kv_copy(i, k_buf, k_out, ko_sem).start()
         kv_copy(i, v_buf, v_out, vo_sem).start()
+        results = []
+        qs = [q_buf[pl.ds(i * rows_kv + u, 16, stride=batch), :].astype(BF16) for u in range(rows_kv)]
+        scores = [
+            lax.dot_general(qs[u], k_buf[i * rows_kv + u], (((1,), (1,)), ((), ())), preferred_element_type=F32)
+            for u in range(rows_kv)
+        ]
         for u in range(rows_kv):
             b = i * rows_kv + u
-            rel = ctx_ref[b] - off
-            q = q_buf[pl.ds(b, 16, stride=batch), :].astype(BF16)
-            s = lax.dot_general(q, k_buf[b], (((1,), (1,)), ((), ())), preferred_element_type=F32) * scale
-            s = jnp.where(pos <= rel, s, NEG_FILL)
+            s = jnp.where(pos <= rels[u], scores[u] * scale, NEG_FILL)
             m = jnp.max(s, axis=-1, keepdims=True)
             w = jnp.exp(s - m)
             l = jnp.sum(w, axis=-1, keepdims=True)
-            acc_ref[pl.ds(b, 16, stride=batch), :] = jnp.dot(w.astype(BF16), v_buf[b], preferred_element_type=F32)
-            m_buf[...] += jnp.where(lane == b, m, 0.0)
-            l_buf[...] += jnp.where(lane == b, l, 0.0)
-        return carry
-
-    lax.fori_loop(0, KV_STEPS, kv_step, 0)
-    stats = jnp.concatenate([m_buf[...], l_buf[...], jnp.zeros((LANES - 32, LANES), F32)], axis=0)
+            m_all = m_all + jnp.where(lane == b, m, 0.0)
+            l_all = l_all + jnp.where(lane == b, l, 0.0)
+            results.append(jnp.dot(w.astype(BF16), v_buf[b], preferred_element_type=F32))
+        for u in range(rows_kv):
+            acc_ref[pl.ds(i * rows_kv + u, 16, stride=batch), :] = results[u]
+        return m_all, l_all
+
+    zero = jnp.zeros((16, LANES), F32)
+    m_all, l_all = lax.fori_loop(0, KV_STEPS, kv_step, (zero, zero))
+    stats = jnp.concatenate([m_all, l_all, jnp.zeros((LANES - 32, LANES), F32)], axis=0)
     ml_ref[...] = stats.T[:batch, :]
     for i in range(KV_STEPS):
         kv_copy(i, k_buf, k_out, ko_sem).wait()
@@ -179,8 +190,8 @@
             rows = pl.ds(i * step, step)
             pltpu.make_async_copy(src.at[rows, :], dst.at[rows, :], sem).start()
 
-    stream(wg_hbm, wg_buf, wg_sem, 8)
-    stream(wu_hbm, wu_buf, wu_sem, 8)
+    stream(wg_hbm, wg_buf, wg_sem, 9)
+    stream(wu_hbm, wu_buf, wu_sem, 9)
     stream(wd_hbm, wd_buf, wd_sem, 9)
 
     pl.semaphore_wait(barrier, 6)
@@ -225,40 +236,45 @@
         for j in range(CHUNKS):
             produce(j)
             cs.append(remote(part.at[1 - core, j], rc_buf.at[ar, j], sc_sem.at[ar, 0, j], rc_sem.at[ar, 0, j], core_dev))
-        for j in range(CHUNKS):
-            cs[j].wait_recv()
-            part[core, j] += rc_buf[ar, j]
-            ys.append(remote(part.at[core, j, pl.ds((1 - y) * 4, 4)], ry_buf.at[ar, j], sy_sem.at[ar, 0, j], ry_sem.at[ar, 0, j], y_dev))
-        for j in range(CHUNKS):
-            ys[j].wait_recv()
-            part[core, j, pl.ds(y * 4, 4)] += ry_buf[ar, j]
+        for j0, j1 in GROUPS:
+            chunks = pl.ds(j0, j1 - j0)
+            for j in range(j0, j1):
+                cs[j].wait_recv()
+                part[core, j] += rc_buf[ar, j]
+            ys.append(remote(part.at[core, chunks, pl.ds((1 - y) * 4, 4)], ry_buf.at[ar, chunks], sy_sem.at[ar, 0, j0], ry_sem.at[ar, 0, j0], y_dev))
+        for i, (j0, j1) in enumerate(GROUPS):
+            chunks = pl.ds(j0, j1 - j0)
+            ys[i].wait_recv()
+            for j in range(j0, j1):
+                part[core, j, pl.ds(y * 4, 4)] += ry_buf[ar, j]
             zs.append([
-                remote(part.at[core, j, y * 4 + peer], rz_buf.at[ar, j, d], sz_sem.at[ar, 0, j, d], rz_sem.at[ar, 0, j, d], {"tp": peer})
+                remote(part.at[core, chunks, y * 4 + peer], rz_buf.at[ar, d, chunks], sz_sem.at[ar, 0, j0, d], rz_sem.at[ar, 0, j0, d], {"tp": peer})
                 for d, peer in enumerate(z_peers)
             ])
         gz, gy, gc = [], [], []
         mine = y * 4 + tp
-        for j in range(CHUNKS):
-            total = part[core, j, mine]
+        for i, (j0, j1) in enumerate(GROUPS):
+            chunks = pl.ds(j0, j1 - j0)
             for d in range(3):
-                zs[j][d].wait_recv()
-                total = total + rz_buf[ar, j, d]
-            full[ar, core, j, mine] = total
+                zs[i][d].wait_recv()
+            for j in range(j0, j1):
+                full[ar, core, j, mine] = part[core, j, mine] + rz_buf[ar, 0, j] + rz_buf[ar, 1, j] + rz_buf[ar, 2, j]
+            block = full.at[ar, core, chunks, mine]
             gz.append([
-                remote(full.at[ar, core, j, mine], full.at[ar, core, j, mine], sz_sem.at[ar, 1, j, d], rz_sem.at[ar, 1, j, d], {"tp": peer})
+                remote(block, block, sz_sem.at[ar, 1, j0, d], rz_sem.at[ar, 1, j0, d], {"tp": peer})
                 for d, peer in enumerate(z_peers)
             ])
-        for j in range(CHUNKS):
+        for i, (j0, j1) in enumerate(GROUPS):
             for d in range(3):
-                gz[j][d].wait_recv()
-            block = full.at[ar, core, j, pl.ds(y * 4, 4)]
-            gy.append(remote(block, block, sy_sem.at[ar, 1, j], ry_sem.at[ar, 1, j], y_dev))
-        for j in range(CHUNKS):
-            gy[j].wait_recv()
-            block = full.at[ar, core, j]
-            gc.append(remote(block, block, sc_sem.at[ar, 1, j], rc_sem.at[ar, 1, j], core_dev))
-        for j in range(CHUNKS):
-            gc[j].wait_recv()
+                gz[i][d].wait_recv()
+            block = full.at[ar, core, pl.ds(j0, j1 - j0), pl.ds(y * 4, 4)]
+            gy.append(remote(block, block, sy_sem.at[ar, 1, j0], ry_sem.at[ar, 1, j0], y_dev))
+        for i, (j0, j1) in enumerate(GROUPS):
+            gy[i].wait_recv()
+            block = full.at[ar, core, pl.ds(j0, j1 - j0)]
+            gc.append(remote(block, block, sc_sem.at[ar, 1, j0], rc_sem.at[ar, 1, j0], core_dev))
+        for copy in gc:
+            copy.wait_recv()
         for copy in cs + ys + gy + gc:
             copy.wait_send()
         for copy in [c for group in zs + gz for c in group]:
@@ -291,14 +307,17 @@
         inv = lax.rsqrt(jnp.sum(sq[r], axis=-1, keepdims=True) / width + EPS)
         for c in range(width // LANES):
             cols = slice(c * LANES, (c + 1) * LANES)
-            n_buf[rows, cols] = (h_buf[rows, cols].astype(F32) * inv * g_ref[:, cols].astype(F32)).astype(BF16)
+            n_buf[rows, cols] = (h_buf[rows, cols].astype(F32) * inv * g_ref[cols].astype(F32)[None, :]).astype(BF16)
 
     pltpu.make_async_copy(wg_hbm, wg_buf, wg_sem).wait()
     pltpu.make_async_copy(wu_hbm, wu_buf, wu_sem).wait()
 
+    def dot_t(a, b):
+        return lax.dot_general(a, b, (((1,), (1,)), ((), ())), preferred_element_type=F32)
+
     def mlp_tile(cols):
-        gate = jnp.dot(n_buf[...], wg_buf[:, cols], preferred_element_type=F32)
-        up = jnp.dot(n_buf[...], wu_buf[:, cols], preferred_element_type=F32)
+        gate = dot_t(n_buf[...], wg_buf[cols, :])
+        up = dot_t(n_buf[...], wu_buf[cols, :])
         act[:, cols] = (jax.nn.silu(gate) * up).astype(BF16)
 
     tiles = ff // 256
@@ -364,8 +383,6 @@
             pltpu.VMEM((16 * batch, head_dim), F32),
             pltpu.VMEM((2 * batch, head_dim), F32),
             pltpu.VMEM((2 * batch, head_dim), F32),
-            pltpu.VMEM((16, LANES), F32),
-            pltpu.VMEM((16, LANES), F32),
             dma((QKV_STEPS,)),
             dma((KV_STEPS,)),
             dma((KV_STEPS,)),
@@ -374,7 +391,7 @@
         ],
         compiler_params=pltpu.CompilerParams(vmem_limit_bytes=60 * 1024 * 1024),
         cost_estimate=pl.CostEstimate(flops=2 * batch * width * cols, bytes_accessed=36 << 20, transcendentals=1 << 19),
-    )(ctx_len, x_in, g_attn.reshape(1, width), cos_t, sin_t, w_qkv, k_cache.reshape(flat), v_cache.reshape(flat))
+    )(ctx_len, x_in, g_attn, cos_t, sin_t, w_qkv, k_cache.reshape(flat), v_cache.reshape(flat))
     return acc.reshape(16, batch, head_dim), ml, k_out.reshape(k_cache.shape), v_out.reshape(v_cache.shape)
 
 
@@ -391,8 +408,8 @@
         out_specs=vmem(),
         scratch_shapes=[
             pltpu.VMEM((w_o.shape[0] + 64, width), BF16),
-            pltpu.VMEM((width, ff), BF16),
-            pltpu.VMEM((width, ff), BF16),
+            pltpu.VMEM((ff, width), BF16),
+            pltpu.VMEM((ff, width), BF16),
             pltpu.VMEM((ff, width), BF16),
             pltpu.VMEM((3, 3, batch, LANES), F32),
             pltpu.VMEM((3, batch, LANES), F32),
@@ -400,7 +417,7 @@
             pltpu.VMEM((2, CHUNKS, UNITS) + unit, F32),
             pltpu.VMEM((2, CHUNKS, UNITS) + unit, F32),
             pltpu.VMEM((2, CHUNKS, 4) + unit, F32),
-            pltpu.VMEM((2, CHUNKS, 3) + unit, F32),
+            pltpu.VMEM((2, 3, CHUNKS) + unit, F32),
             pltpu.VMEM((2, 2, CHUNKS, UNITS) + unit, F32),
             pltpu.VMEM((batch, width), BF16),
             pltpu.VMEM((batch, width), BF16),
@@ -415,7 +432,7 @@
             collective_id=0, has_side_effects=True, vmem_limit_bytes=67_043_328
         ),
         cost_estimate=pl.CostEstimate(flops=6 * batch * width * ff, bytes_accessed=58 << 20, transcendentals=1 << 17),
-    )(acc, ml, x_in, g_mlp.reshape(1, width), w_o, w_gate, w_up, w_down)
+    )(acc, ml, x_in, g_mlp, w_o, w_gate.T, w_up.T, w_down)
 
 
 def solution(mesh):

time: 142 us -> 95.1 us (0.67)
  local copies, waits for them, and re-layouts: 50.3 us -> 1.72 us
  Pallas kernels: 87.9 us -> 90.2 us
    unnamed x3 -> x1, local copies, waits for them, and re-layouts: 47.7 us -> 1.72 us
    pallas_call x1, Pallas kernels: 67.9 us -> 76 us  [tail_call(): pl.pallas_call(tail_kernel, name='tail', out_shape=jax.ShapeDtypeStruct((...]
    pallas_call x1, Pallas kernels: 20 us -> 14.3 us  [attention_call(): pl.pallas_call(attention_kernel, name='attention', out_shape=(jax.ShapeDt...]
    reshape x2 -> x0, local copies, waits for them, and re-layouts: 2.64 us -> none  [the longest x1 1.33 us: attention_call(): g_attn.reshape(1, width)]
where the time goes in v2:
time: 95.1 us; the launch traced here: 94 us
  Pallas kernels  90.2 us (95%)
  local copies, waits for them, and re-layouts  1.72 us (2%)
  other arithmetic  1.43 us (2%)
    pallas_call x1, Pallas kernels, tail_call(): pl.pallas_call(tail_kernel, name='tail', out_shape=jax.ShapeDtypeStruct((...  76 us
    pallas_call x1, Pallas kernels, attention_call(): pl.pallas_call(attention_kernel, name='attention', out_shape=(jax.ShapeDt...  14.3 us

profile of v2, /device:TPU:0, one launch (start us, length us, event | category | flops | bytes accessed | tf_op | source)
XLA Modules:
  0.0 94.0 jit_solution(18254870266274047042)
XLA Ops:
  0.6 0.7 convert_element_type.11
  1.3 0.8 fusion
  2.1 14.3 %attention.1 = (f32[512,128]{1,0:T(8,128)}, f32[32,128]{1,0:T(8,128)}, bf16[32,512,128]{2,1,0:T(8,128)(2,1)}, bf16[32,512,128]{2,1,0:T(8,128)(2,1)}) custom-call(s32[32]{0:T(128)} %ctx_ref.1, bf16[32,5120]{1,0:T(8,128)(2,1)} %x_ref.3, bf16[5120]{0:T(1024)(128)(2,1)} %g_ref.2, f32[32,128]{1,0:T(8,128)} %get-tuple-element.12.cos_ref, ...), custom_call_target="tpu_custom_call" | custom-call | flops 587202560 | bytes 37748736 | tf_op jit(solution)/shard_map/attention/pallas_call | solution.py:366
  16.3 76.0 %tail.1 = bf16[32,5120]{1,0:T(8,128)(2,1)} custom-call(f32[16,32,128]{2,1,0:T(8,128)} %bitcast.11, f32[32,128]{1,0:T(8,128)} %get-tuple-element.8.ml_ref, bf16[32,5120]{1,0:T(8,128)(2,1)} %x_ref.3, bf16[5120]{0:T(1024)(128)(2,1)} %g_ref.3, bf16[320,5120]{1,0:T(8,128)(2,1)} %wo_hbm.1, bf16[1728,5120]{1,0:T(8,128)(2,1)} %bitcast.7, ...), custom_call_target="tpu_custom_call" | custom-call | flops 1698693120 | bytes 60817408 | tf_op jit(solution)/shard_map/tail/pallas_call | solution.py:403
  92.3 1.7 %copy.15 = bf16[32,5120]{1,0:T(8,128)(2,1)} copy(bf16[32,5120]{1,0:T(8,128)(2,1)} %tail.1) | data formatting | bytes 655360
  (1 shorter events, 0.0 us)

commit v3 on v2

--- a/solution.py
+++ b/solution.py
@@ -14,9 +14,10 @@
 HALF = 16
 MESH = pl.DeviceIdType.MESH
 QKV_STEPS = 10
+PIECES = 9
 KV_STEPS = 4
 CHUNKS = 5
-GROUPS = ((0, 3), (3, 5))
+GROUPS = ((0, 1), (1, 2), (2, 3), (3, 4), (4, 5))
 UNITS = 8
 F32 = jnp.float32
 BF16 = jnp.bfloat16
@@ -184,16 +185,17 @@
     gap = pl.multiple_of((1 - odd) * rows_o, 64)
     wo_buf[pl.ds(gap, 64), :] = jnp.zeros((64, width), BF16)
 
-    def stream(src, dst, sem, pieces):
-        step = src.shape[0] // pieces
-        for i in range(pieces):
-            rows = pl.ds(i * step, step)
-            pltpu.make_async_copy(src.at[rows, :], dst.at[rows, :], sem).start()
-
-    stream(wg_hbm, wg_buf, wg_sem, 9)
-    stream(wu_hbm, wu_buf, wu_sem, 9)
-    stream(wd_hbm, wd_buf, wd_sem, 9)
-
+    pieces = []
+    for src, dst, sem in ((wg_hbm, wg_buf, wg_sem), (wu_hbm, wu_buf, wu_sem), (wd_hbm, wd_buf, wd_sem)):
+        step = src.shape[0] // PIECES
+        for i in range(PIECES):
+            pieces.append((src.at[pl.ds(i * step, step), :], dst.at[pl.ds(i * step, step), :], sem))
+
+    def pump(count):
+        for _ in range(min(count, len(pieces))):
+            pltpu.make_async_copy(*pieces.pop(0)).start()
+
+    pump(2)
     pl.semaphore_wait(barrier, 6)
 
     sends = []
@@ -208,6 +210,7 @@
             )
             copy.start()
             sends.append(copy)
+    pump(6)
     for copy in sends:
         copy.wait_recv()
     head0 = (5 * kvp) // 2
@@ -231,17 +234,23 @@
     core_dev = {"kvp": kv_peers[0]}
     y_dev = {"kvp": kv_peers[1]}
 
-    def all_reduce(ar, produce):
+    def all_reduce(ar, produce, lag):
         cs, ys, zs, started = [], [], [], []
-        for j in range(CHUNKS):
-            produce(j)
-            cs.append(remote(part.at[1 - core, j], rc_buf.at[ar, j], sc_sem.at[ar, 0, j], rc_sem.at[ar, 0, j], core_dev))
-        for j0, j1 in GROUPS:
+        def core_sum(j0, j1):
             chunks = pl.ds(j0, j1 - j0)
             for j in range(j0, j1):
                 cs[j].wait_recv()
                 part[core, j] += rc_buf[ar, j]
             ys.append(remote(part.at[core, chunks, pl.ds((1 - y) * 4, 4)], ry_buf.at[ar, chunks], sy_sem.at[ar, 0, j0], ry_sem.at[ar, 0, j0], y_dev))
+
+        for j in range(CHUNKS):
+            produce(j)
+            cs.append(remote(part.at[1 - core, j], rc_buf.at[ar, j], sc_sem.at[ar, 0, j], rc_sem.at[ar, 0, j], core_dev))
+            if j - lag >= 0:
+                core_sum(*GROUPS[j - lag])
+        for j in range(CHUNKS - lag, CHUNKS):
+            core_sum(*GROUPS[j])
+        pump(3)
         for i, (j0, j1) in enumerate(GROUPS):
             chunks = pl.ds(j0, j1 - j0)
             ys[i].wait_recv()
@@ -251,6 +260,7 @@
                 remote(part.at[core, chunks, y * 4 + peer], rz_buf.at[ar, d, chunks], sz_sem.at[ar, 0, j0, d], rz_sem.at[ar, 0, j0, d], {"tp": peer})
                 for d, peer in enumerate(z_peers)
             ])
+            pump(1)
         gz, gy, gc = [], [], []
         mine = y * 4 + tp
         for i, (j0, j1) in enumerate(GROUPS):
@@ -264,11 +274,14 @@
                 remote(block, block, sz_sem.at[ar, 1, j0, d], rz_sem.at[ar, 1, j0, d], {"tp": peer})
                 for d, peer in enumerate(z_peers)
             ])
+            pump(1)
         for i, (j0, j1) in enumerate(GROUPS):
             for d in range(3):
                 gz[i][d].wait_recv()
             block = full.at[ar, core, pl.ds(j0, j1 - j0), pl.ds(y * 4, 4)]
             gy.append(remote(block, block, sy_sem.at[ar, 1, j0], ry_sem.at[ar, 1, j0], y_dev))
+            pump(1)
+        pump(len(pieces))
         for i, (j0, j1) in enumerate(GROUPS):
             gy[i].wait_recv()
             block = full.at[ar, core, pl.ds(j0, j1 - j0)]
@@ -291,7 +304,7 @@
         cols = slice(j * UNITS * LANES, (j + 1) * UNITS * LANES)
         store_part(j, 0, jnp.dot(a_buf[...], wo_buf[:, cols], preferred_element_type=F32))
 
-    all_reduce(0, produce_o)
+    all_reduce(0, produce_o, 5)
 
     sq = [jnp.zeros((HALF, LANES), F32) for _ in range(2)]
     for c in range(width // LANES):
@@ -337,7 +350,7 @@
             cols = slice((2 * j + half) * 512, (2 * j + half + 1) * 512)
             store_part(j, half * 4, jnp.dot(act[...], wd_buf[:, cols], preferred_element_type=F32))
 
-    all_reduce(1, produce_down)
+    all_reduce(1, produce_down, 2)
 
     for c in range(width // LANES):
         j, u = divmod(c, UNITS)

time: 95.1 us -> 81.2 us (0.85)
  Pallas kernels: 90.2 us -> 77.2 us
    pallas_call x1, Pallas kernels: 76 us -> 62.9 us  [tail_call(): pl.pallas_call(tail_kernel, name='tail', out_shape=jax.ShapeDtypeStruct((...]
where the time goes in v3:
time: 81.2 us; the launch traced here: 81 us
  Pallas kernels  77.2 us (95%)
  local copies, waits for them, and re-layouts  1.72 us (2%)
  other arithmetic  1.43 us (2%)
    pallas_call x1, Pallas kernels, tail_call(): pl.pallas_call(tail_kernel, name='tail', out_shape=jax.ShapeDtypeStruct((...  62.9 us
    pallas_call x1, Pallas kernels, attention_call(): pl.pallas_call(attention_kernel, name='attention', out_shape=(jax.ShapeDt...  14.3 us
    unnamed x1, local copies, waits for them, and re-layouts  1.72 us

profile of v3, /device:TPU:0, one launch (start us, length us, event | category | flops | bytes accessed | tf_op | source)
XLA Modules:
  0.0 81.0 jit_solution(6948134308968138914)
XLA Ops:
  0.6 0.7 convert_element_type.11
  1.3 0.8 fusion
  2.1 14.3 %attention.1 = (f32[512,128]{1,0:T(8,128)}, f32[32,128]{1,0:T(8,128)}, bf16[32,512,128]{2,1,0:T(8,128)(2,1)}, bf16[32,512,128]{2,1,0:T(8,128)(2,1)}) custom-call(s32[32]{0:T(128)} %ctx_ref.1, bf16[32,5120]{1,0:T(8,128)(2,1)} %x_ref.3, bf16[5120]{0:T(1024)(128)(2,1)} %g_ref.2, f32[32,128]{1,0:T(8,128)} %get-tuple-element.12.cos_ref, ...), custom_call_target="tpu_custom_call" | custom-call | flops 587202560 | bytes 37748736 | tf_op jit(solution)/shard_map/attention/pallas_call | solution.py:379
  16.3 62.9 %tail.1 = bf16[32,5120]{1,0:T(8,128)(2,1)} custom-call(f32[16,32,128]{2,1,0:T(8,128)} %bitcast.11, f32[32,128]{1,0:T(8,128)} %get-tuple-element.8.ml_ref, bf16[32,5120]{1,0:T(8,128)(2,1)} %x_ref.3, bf16[5120]{0:T(1024)(128)(2,1)} %g_ref.3, bf16[320,5120]{1,0:T(8,128)(2,1)} %wo_hbm.1, bf16[1728,5120]{1,0:T(8,128)(2,1)} %bitcast.7, ...), custom_call_target="tpu_custom_call" | custom-call | flops 1698693120 | bytes 60817408 | tf_op jit(solution)/shard_map/tail/pallas_call | solution.py:416
  79.3 1.7 %copy.15 = bf16[32,5120]{1,0:T(8,128)(2,1)} copy(bf16[32,5120]{1,0:T(8,128)(2,1)} %tail.1) | data formatting | bytes 655360
  (1 shorter events, 0.0 us)
